TPU v7x, 256 devices: a whole 4x4x8 slice. The times are simulated.
256 devices in a mesh: ep: 64 (over z, y, core), fsdp: 4 (over x).
Axes of the slice: x: 4, y: 4, z: 8, core: 2. Of those that a mesh axis runs over, the one named last changes fastest.
Arguments:
- train_gate: float32 [64, 2048, 1024], P('ep', 'fsdp'), may hold values from -0.1875 to 0.1875
- other_gate: bfloat16 [64, 2048, 1024], P('ep', 'fsdp'), may hold values from -0.0625 to 0.0625
- train_up: float32 [64, 2048, 1024], P('ep', 'fsdp'), may hold values from -0.1875 to 0.1875
- other_up: bfloat16 [64, 2048, 1024], P('ep', 'fsdp'), may hold values from -0.0625 to 0.0625
- router_weight: float32 [2048, 64], P('fsdp', 'ep'), may hold values from -0.125 to 0.125
- router_gain: float32 [2048], P('fsdp'), may hold values from 0.25 to 1.75
Outputs:
- ready_gate: bfloat16 [64, 2048, 1024], P('ep')
- ready_up: bfloat16 [64, 2048, 1024], P('ep')
- scale_gate: float32 [64, 1024], P('ep')
- scale_up: float32 [64, 1024], P('ep')
- serve_router: bfloat16 [2048, 64], replicated
All inputs are finite; a program needn't handle non-finite values.
Results may differ from a plain program's by a relative error of at most 0.001.
Values may be sent and summed in bfloat16 or wider, within the bound.
A program may use at most 64 MiB of HBM per device.

v0:
```python
import jax
import jax.numpy as jnp
from jax import lax
from jax.sharding import PartitionSpec as P


def copy_for_each(value, axis):
    copies = jnp.broadcast_to(value, (lax.axis_size(axis), *value.shape))
    return lax.all_to_all(copies, axis, split_axis=0, concat_axis=0, tiled=True)


def over_copies(value, axis):
    return copy_for_each(value, axis).sum(axis=0)


def packed_total(arrays, axis):
    flat, at, outs = (jnp.concatenate([a.reshape(-1) for a in arrays]), 0, [])
    so_far = over_copies(flat, axis)
    for a in arrays:
        outs.append(so_far[at : at + a.size].reshape(a.shape))
        at += a.size
    return tuple(outs)


def side_by_side(arrays, axis, dim, along):
    widths = [a.shape[along] for a in arrays]
    both = jnp.concatenate(arrays, axis=along)
    out = lax.all_gather(both, axis, axis=dim, tiled=True)
    return tuple(jnp.split(out, [sum(widths[:k]) for k in range(1, len(widths))], axis=along))


def joined_along(blocks, dim):
    dims = list(blocks.shape[1:])
    dims[dim] *= blocks.shape[0]
    return jnp.moveaxis(blocks, 0, dim).reshape(dims)


def gather_directly(value, axis, dim):
    return joined_along(copy_for_each(value, axis), dim)


def body(train_gate, other_gate, train_up, other_up, router_weight, router_gain):
    latest_gate = train_gate + other_gate.astype(jnp.float32)
    latest_up = train_up + other_up.astype(jnp.float32)
    total_gate, total_up = packed_total(
        (jnp.sum(latest_gate * latest_gate, axis=1), jnp.sum(latest_up * latest_up, axis=1)), "fsdp"
    )
    scale_gate = jnp.sqrt(total_gate)
    scale_up = jnp.sqrt(total_up)
    narrow_gate, narrow_up = (
        (latest_gate / jnp.expand_dims(scale_gate, 1)).astype(jnp.bfloat16),
        (latest_up / jnp.expand_dims(scale_up, 1)).astype(jnp.bfloat16),
    )
    ready_gate, ready_up = side_by_side((narrow_gate, narrow_up), "fsdp", 1, 0)
    part_router = (router_weight * router_gain[:, None]).astype(jnp.bfloat16)
    row_router = lax.all_gather(part_router, "fsdp", axis=0, tiled=True)
    serve_router = gather_directly(row_router, "ep", 1)
    return (ready_gate, ready_up, scale_gate, scale_up, serve_router)


def solution(mesh):
    placed = (
        P("ep", "fsdp", None),
        P("ep", "fsdp", None),
        P("ep", "fsdp", None),
        P("ep", "fsdp", None),
        P("fsdp", "ep"),
        P("fsdp"),
    )
    return jax.shard_map(
        body,
        mesh=mesh,
        in_specs=placed,
        out_specs=(P("ep", None, None), P("ep", None, None), P("ep", None), P("ep", None), P()),
        check_vma=False,
    )
```

profile of v0, /device:TPU:1, one launch (start us, length us, event | category | flops | bytes accessed | tf_op | source)
XLA Modules:
  0.0 124.7 jit_solution(4241068722860294294)
XLA Ops:
  7.2 0.0 copy-start
  7.2 0.0 copy-start.2
  7.2 0.0 all-gather.2.cloned.1.call-start
  7.2 3.6 %multiply_reduce_fusion = (f32[1024]{0:T(1024)S(1)}, f32[1024]{0:T(1024)S(1)}) fusion(f32[1,512,1024]{2,1,0:T(8,128)} %param.8, bf16[1,512,1024]{2,1,0:T(8,128)(2,1)} %param.9, f32[1,512,1024]{2,1,0:T(8,128)} %param.6, bf16[1,512,1024]{2,1,0:T(8,128)(2,1)} %param.7), kind=kLoop, calls=%fused_computation.3 | loop fusion | flops 4192256 | bytes 6299648 | tf_op jit(solution)/shard_map/reduce_sum | solution.py:46
  10.9 8.9 %all_to_all.11 = f32[4,1,2048]{2,1,0:T(1,128)S(1)} all-to-all(f32[4,1,2048]{2,1,0:T(1,128)S(1)} %broadcast_in_dim.11), channel_id=1, replica_groups=mesh['ep'=64,'fsdp'=4] {'fsdp'}, dimensions={0} | all-to-all | bytes 65536 | tf_op jit(solution)/shard_map/all_to_all | solution.py:9
  19.9 0.0 copy-start.5
  19.9 0.0 copy-start.4
  19.9 0.0 copy-done
  19.9 0.0 copy-done.2
  19.9 0.0 copy-start.1
  19.9 0.0 copy-start.3
  20.0 0.4 divide_convert_fusion
  20.3 0.1 copy-done.5
  20.5 0.0 copy-done.4
  20.5 1.0 copy-done.1
  21.5 0.3 copy-done.3
  21.8 0.4 divide_convert_fusion.1
  22.2 1.5 %pad_maximum_fusion = bf16[2,512,1024]{2,1,0:T(8,128)(2,1)} fusion(bf16[1,512,1024]{2,1,0:T(8,128)(2,1)S(1)} %divide_convert_fusion, bf16[1,512,1024]{2,1,0:T(8,128)(2,1)S(1)} %divide_convert_fusion.1), kind=kLoop, calls=%fused_computation | loop fusion | flops 1048576 | bytes 4194304 | tf_op jit(solution)/shard_map/concatenate | solution.py:27
  23.7 0.0 copy-start.6
  23.7 0.0 copy-start.7
  23.7 0.0 all-gather.2.cloned.1.call-update
  23.7 0.7 copy-done.6
  24.4 0.0 copy-done.7
  24.4 8.1 %all_gather.9 = bf16[2048,1]{0,1:T(2,128)(2,1)S(1)} all-gather(bf16[512,1]{0,1:T(2,128)(2,1)S(1)} %multiply_convert_fusion), channel_id=1, replica_groups=mesh['ep'=64,'fsdp'=4] {'fsdp'}, dimensions={0}, use_global_device_ids=true | all-gather | bytes 5120 | tf_op jit(solution)/shard_map/all_gather | solution.py:56
  32.6 0.3 broadcast_bitcast_fusion
  32.8 0.5 broadcast.9
  33.4 2.2 %reduce.4 = bf16[64,2048]{1,0:T(8,128)(2,1)S(1)} reduce(bf16[64,1,2048]{2,1,0:T(2,128)(2,1)S(1)} %broadcast_bitcast_fusion, bf16[]{:T(256)} %broadcast.9), dimensions={1}, to_apply=%broadcast_bitcast_fusion.reduce_sub_computation | reduce | bytes 524290
  35.5 0.2 reshape.38
  35.7 28.9 %all_to_all.12 = bf16[64,2,1024]{2,1,0:T(2,128)(2,1)S(1)} all-to-all(bf16[64,2,1024]{2,1,0:T(2,128)(2,1)S(1)} %reshape.38), channel_id=1, replica_groups=mesh['ep'=64,'fsdp'=4] {'ep'}, dimensions={0} | all-to-all | bytes 524288 | tf_op jit(solution)/shard_map/all_to_all | solution.py:9
  64.6 0.2 reshape.39
  64.9 0.9 copy.19
  65.7 46.1 %all-gather.2.cloned.1.call-done = bf16[2,2048,1024]{2,1,0:T(8,128)(2,1)} async-done(((bf16[2,512,1024]{2,1,0:T(8,128)(2,1)}), bf16[2,2048,1024]{2,1,0:T(8,128)(2,1)}) %all-gather.2.cloned.1.call-update) | async-done | bytes 8388624 | tf_op jit(solution)/shard_map/all_gather | solution.py:28
  111.8 6.0 %fusion = (bf16[1,2048,1024]{2,1,0:T(8,128)(2,1)}, bf16[1,2048,1024]{2,1,0:T(8,128)(2,1)}) fusion(bf16[2,2048,1024]{2,1,0:T(8,128)(2,1)} %all-gather.2.cloned.1.call-done), kind=kLoop, calls=%fused_computation.12 | loop fusion | bytes 16777216 | tf_op jit(solution)/shard_map/split | solution.py:29
  (6 shorter events, 0.1 us)
Async XLA Ops:
  7.2 12.7 %copy-start = (f32[1,512,1024]{2,1,0:T(8,128)S(1)}, f32[1,512,1024]{2,1,0:T(8,128)}, u32[]{:S(2)}) copy-start(f32[1,512,1024]{2,1,0:T(8,128)} %param.8) | copy-start | bytes 6291460
  7.2 12.7 %copy-start.2 = (bf16[1,512,1024]{2,1,0:T(8,128)(2,1)S(1)}, bf16[1,512,1024]{2,1,0:T(8,128)(2,1)}, u32[]{:S(2)}) copy-start(bf16[1,512,1024]{2,1,0:T(8,128)(2,1)} %param.9) | copy-start | bytes 3145732
  7.2 104.7 %all-gather.2.cloned.1.call-start = ((), (), s32[]{:S(2)}) async-start(), calls=%async_computation.2 | async-start | bytes 10485760 | tf_op jit(solution)/shard_map/all_gather | solution.py:28
  19.9 0.6 copy-start.5
  19.9 0.6 copy-start.4
  19.9 1.6 %copy-start.1 = (f32[1,512,1024]{2,1,0:T(8,128)S(1)}, f32[1,512,1024]{2,1,0:T(8,128)}, u32[]{:S(2)}) copy-start(f32[1,512,1024]{2,1,0:T(8,128)} %param.6) | copy-start | bytes 6291460
  19.9 1.8 %copy-start.3 = (bf16[1,512,1024]{2,1,0:T(8,128)(2,1)S(1)}, bf16[1,512,1024]{2,1,0:T(8,128)(2,1)}, u32[]{:S(2)}) copy-start(bf16[1,512,1024]{2,1,0:T(8,128)(2,1)} %param.7) | copy-start | bytes 3145732
  23.7 0.7 copy-start.6
  23.7 0.7 copy-start.7
Sparse Core Ops, SparseCore 0:
  23.8 87.9 all-gather.1
where the time goes:
time: 125 us
  waiting for transfers between devices  46.1 us (37%)
  blocking collectives  46 us (37%)
  between operations  14.2 us (11%)
  local copies, waits for them, and re-layouts  10.2 us (8%)
  other arithmetic  8.13 us (7%)
    all_gather x1, waiting for transfers between devices, side_by_side(): out = lax.all_gather(both, axis, axis=dim, tiled=True)  46.1 us
    all_to_all x2, blocking collectives, copy_for_each(): return lax.all_to_all(copies, axis, split_axis=0, concat_axis=0, tiled=True)  37.9 us
    all_gather x1, blocking collectives, body(): row_router = lax.all_gather(part_router, 'fsdp', axis=0, tiled=True)  8.13 us
    split x1, local copies, waits for them, and re-layouts, side_by_side(): jnp.split(out, [sum(widths[:k]) for k in range(1, len(widths))], axis=along)  6.02 us
    reduce_sum x1, other arithmetic, body(): jnp.sum(latest_up * latest_up, axis=1)  3.63 us
    unnamed x20, local copies, waits for them, and re-layouts  3.34 us
  transfers between devices with their start and end apart: 1, of which 1 were waited for; matrix products, arithmetic and copies ran while one was open for 3% of the time, Pallas kernels for 0%

commit v1 on v0

--- a/solution.py
+++ b/solution.py
@@ -2,6 +2,12 @@
 import jax.numpy as jnp
 from jax import lax
 from jax.sharding import PartitionSpec as P
+
+
+def in_order(pieces, dim):
+    pieces = jnp.moveaxis(pieces, 0, dim)
+    shape = pieces.shape
+    return pieces.reshape(*shape[:dim], shape[dim] * shape[dim + 1], *shape[dim + 2 :])
 
 
 def copy_for_each(value, axis):
@@ -53,7 +59,19 @@
     )
     ready_gate, ready_up = side_by_side((narrow_gate, narrow_up), "fsdp", 1, 0)
     part_router = (router_weight * router_gain[:, None]).astype(jnp.bfloat16)
-    row_router = lax.all_gather(part_router, "fsdp", axis=0, tiled=True)
+    size = lax.axis_size("fsdp")
+    pairs = [(i, (i + 1) % size) for i in range(size)]
+    back = [(b, a_2) for a_2, b in pairs]
+    lower, upper = ([], [])
+    for step in range(size - 1):
+        if step % 2 == 0:
+            lower.append(lax.ppermute(lower[-1] if lower else part_router, "fsdp", pairs))
+        else:
+            upper.append(lax.ppermute(upper[-1] if upper else part_router, "fsdp", back))
+    pieces = jnp.stack([*lower[::-1], part_router, *upper])
+    shift = lax.axis_index("fsdp") - len(lower)
+    pieces = pieces[(jnp.arange(size) - shift) % size]
+    row_router = in_order(pieces, 0)
     serve_router = gather_directly(row_router, "ep", 1)
     return (ready_gate, ready_up, scale_gate, scale_up, serve_router)
 

time: 125 us -> 125 us (level)
  blocking collectives: 46 us -> 38.1 us
  waiting for transfers between devices: 46.1 us -> 51.9 us
  starting transfers between devices: 0.04 us -> 1.57 us
    all_gather x1 -> x0, blocking collectives: 8.13 us -> none  [body(): row_router = lax.all_gather(part_router, 'fsdp', axis=0, tiled=True)]
    ppermute x0 -> x3, waiting for transfers between devices: none -> 6.68 us  [the longest x2 6.68 us: body(): lax.ppermute(lower[-1] if lower else part_router, 'fsdp', pairs)]
    ppermute x0 -> x3, starting transfers between devices: none -> 1.53 us  [the longest x1 0.95 us: body(): lax.ppermute(upper[-1] if upper else part_router, 'fsdp', back)]
    unnamed x20 -> x21, local copies, waits for them, and re-layouts: 3.34 us -> 3.35 us
  transfers between devices with their start and end apart: 1 -> 4, of which waited for: 1 -> 3; matrix products, arithmetic and copies ran while one was open for 3% -> 4% of each run, Pallas kernels for 0% -> 0%
where the time goes in v1:
time: 125 us
  waiting for transfers between devices  51.9 us (42%)
  blocking collectives  38.1 us (30%)
  between operations  14.2 us (11%)
  local copies, waits for them, and re-layouts  10.8 us (9%)
  other arithmetic  8.13 us (7%)
  starting transfers between devices  1.57 us (1%)
    all_gather x1, waiting for transfers between devices, side_by_side(): out = lax.all_gather(both, axis, axis=dim, tiled=True)  45.2 us
    all_to_all x2, blocking collectives, copy_for_each(): return lax.all_to_all(copies, axis, split_axis=0, concat_axis=0, tiled=True)  38.1 us
    ppermute x2, waiting for transfers between devices, body(): lax.ppermute(lower[-1] if lower else part_router, 'fsdp', pairs)  6.68 us
    split x1, local copies, waits for them, and re-layouts, side_by_side(): jnp.split(out, [sum(widths[:k]) for k in range(1, len(widths))], axis=along)  6.02 us
    reduce_sum x1, other arithmetic, body(): jnp.sum(latest_up * latest_up, axis=1)  3.63 us
    unnamed x21, local copies, waits for them, and re-layouts  3.35 us
  transfers between devices with their start and end apart: 4, of which 3 were waited for; matrix products, arithmetic and copies ran while one was open for 4% of the time, Pallas kernels for 0%

profile of v1, /device:TPU:1, one launch (start us, length us, event | category | flops | bytes accessed | tf_op | source)
XLA Modules:
  0.0 124.7 jit_solution(10926996857640835054)
XLA Ops:
  7.2 0.0 copy-start
  7.2 0.0 copy-start.2
  7.2 0.0 all-gather.2.cloned.1.call-start
  7.2 3.6 %multiply_reduce_fusion = (f32[1024]{0:T(1024)S(1)}, f32[1024]{0:T(1024)S(1)}) fusion(f32[1,512,1024]{2,1,0:T(8,128)} %param.8, bf16[1,512,1024]{2,1,0:T(8,128)(2,1)} %param.9, f32[1,512,1024]{2,1,0:T(8,128)} %param.6, bf16[1,512,1024]{2,1,0:T(8,128)(2,1)} %param.7), kind=kLoop, calls=%fused_computation.4 | loop fusion | flops 4192256 | bytes 6299648 | tf_op jit(solution)/shard_map/reduce_sum | solution.py:52
  10.9 8.9 %all_to_all.11 = f32[4,1,2048]{2,1,0:T(1,128)S(1)} all-to-all(f32[4,1,2048]{2,1,0:T(1,128)S(1)} %broadcast_in_dim.12), channel_id=1, replica_groups=mesh['ep'=64,'fsdp'=4] {'fsdp'}, dimensions={0} | all-to-all | bytes 65536 | tf_op jit(solution)/shard_map/all_to_all | solution.py:15
  19.9 0.0 copy-start.5
  19.9 0.0 copy-start.4
  19.9 0.0 copy-done
  19.9 0.0 copy-done.2
  19.9 0.0 copy-start.1
  19.9 0.0 copy-start.3
  20.0 0.4 divide_convert_fusion
  20.3 0.1 copy-done.5
  20.5 0.0 copy-done.4
  20.5 1.0 copy-done.1
  21.5 0.3 copy-done.3
  21.8 0.4 divide_convert_fusion.1
  22.2 1.5 %pad_maximum_fusion = bf16[2,512,1024]{2,1,0:T(8,128)(2,1)} fusion(bf16[1,512,1024]{2,1,0:T(8,128)(2,1)S(1)} %divide_convert_fusion, bf16[1,512,1024]{2,1,0:T(8,128)(2,1)S(1)} %divide_convert_fusion.1), kind=kLoop, calls=%fused_computation.1 | loop fusion | flops 1048576 | bytes 4194304 | tf_op jit(solution)/shard_map/concatenate | solution.py:33
  23.7 0.0 copy-start.6
  23.7 0.0 copy-start.7
  23.7 0.0 all-gather.2.cloned.1.call-update
  23.7 0.7 copy-done.6
  24.4 0.0 copy-done.7
  24.4 0.9 collective-permute-start.2
  25.4 0.6 collective-permute-start
  25.9 3.1 %collective-permute-done = bf16[512,1]{0,1:T(2,128)(2,1)S(1)} collective-permute-done((bf16[512,1]{0,1:T(2,128)(2,1)S(1)}, bf16[512,1]{0,1:T(2,128)(2,1)S(1)}, u32[]{:S(2)}, u32[]{:S(2)}) %collective-permute-start) | collective-permute-done | bytes 1056 | tf_op jit(solution)/shard_map/ppermute | solution.py:68
  29.0 0.0 collective-permute-start.1
  29.0 0.0 collective-permute-done.2
  29.0 3.6 %collective-permute-done.1 = bf16[512,1]{0,1:T(2,128)(2,1)S(1)} collective-permute-done((bf16[512,1]{0,1:T(2,128)(2,1)S(1)}, bf16[512,1]{0,1:T(2,128)(2,1)S(1)}, u32[]{:S(2)}, u32[]{:S(2)}) %collective-permute-start.1) | collective-permute-done | bytes 1056 | tf_op jit(solution)/shard_map/ppermute | solution.py:68
  32.7 0.6 gather_fusion
  33.2 0.3 broadcast_bitcast_fusion
  33.5 0.5 broadcast.77
  34.0 2.2 %reduce.3 = bf16[64,2048]{1,0:T(8,128)(2,1)S(1)} reduce(bf16[64,1,2048]{2,1,0:T(2,128)(2,1)S(1)} %broadcast_bitcast_fusion, bf16[]{:T(256)} %broadcast.77), dimensions={1}, to_apply=%broadcast_bitcast_fusion.reduce_sub_computation | reduce | bytes 524290
  36.2 0.2 reshape.102
  36.4 29.2 %all_to_all.12 = bf16[64,2,1024]{2,1,0:T(2,128)(2,1)S(1)} all-to-all(bf16[64,2,1024]{2,1,0:T(2,128)(2,1)S(1)} %reshape.102), channel_id=1, replica_groups=mesh['ep'=64,'fsdp'=4] {'ep'}, dimensions={0} | all-to-all | bytes 524288 | tf_op jit(solution)/shard_map/all_to_all | solution.py:15
  65.6 0.2 reshape.103
  65.8 0.9 copy.20
  66.7 45.2 %all-gather.2.cloned.1.call-done = bf16[2,2048,1024]{2,1,0:T(8,128)(2,1)} async-done(((bf16[2,512,1024]{2,1,0:T(8,128)(2,1)}), bf16[2,2048,1024]{2,1,0:T(8,128)(2,1)}) %all-gather.2.cloned.1.call-update) | async-done | bytes 8388624 | tf_op jit(solution)/shard_map/all_gather | solution.py:34
  111.8 6.0 %fusion.2 = (bf16[1,2048,1024]{2,1,0:T(8,128)(2,1)}, bf16[1,2048,1024]{2,1,0:T(8,128)(2,1)}) fusion(bf16[2,2048,1024]{2,1,0:T(8,128)(2,1)} %all-gather.2.cloned.1.call-done), kind=kLoop, calls=%fused_computation.21 | loop fusion | bytes 16777216 | tf_op jit(solution)/shard_map/split | solution.py:35
  (9 shorter events, 0.1 us)
Async XLA Ops:
  7.2 12.7 %copy-start = (f32[1,512,1024]{2,1,0:T(8,128)S(1)}, f32[1,512,1024]{2,1,0:T(8,128)}, u32[]{:S(2)}) copy-start(f32[1,512,1024]{2,1,0:T(8,128)} %param.8) | copy-start | bytes 6291460
  7.2 12.7 %copy-start.2 = (bf16[1,512,1024]{2,1,0:T(8,128)(2,1)S(1)}, bf16[1,512,1024]{2,1,0:T(8,128)(2,1)}, u32[]{:S(2)}) copy-start(bf16[1,512,1024]{2,1,0:T(8,128)(2,1)} %param.9) | copy-start | bytes 3145732
  7.2 104.7 %all-gather.2.cloned.1.call-start = ((), (), s32[]{:S(2)}) async-start(), calls=%async_computation.2 | async-start | bytes 10485760 | tf_op jit(solution)/shard_map/all_gather | solution.py:34
  19.9 0.6 copy-start.5
  19.9 0.6 copy-start.4
  19.9 1.6 %copy-start.1 = (f32[1,512,1024]{2,1,0:T(8,128)S(1)}, f32[1,512,1024]{2,1,0:T(8,128)}, u32[]{:S(2)}) copy-start(f32[1,512,1024]{2,1,0:T(8,128)} %param.6) | copy-start | bytes 6291460
  19.9 1.8 %copy-start.3 = (bf16[1,512,1024]{2,1,0:T(8,128)(2,1)S(1)}, bf16[1,512,1024]{2,1,0:T(8,128)(2,1)}, u32[]{:S(2)}) copy-start(bf16[1,512,1024]{2,1,0:T(8,128)(2,1)} %param.7) | copy-start | bytes 3145732
  23.7 0.7 copy-start.6
  23.7 0.7 copy-start.7
  24.4 4.6 %collective-permute-start.2 = (bf16[512,1]{0,1:T(2,128)(2,1)S(1)}, bf16[512,1]{0,1:T(2,128)(2,1)S(1)}, u32[]{:S(2)}, u32[]{:S(2)}) collective-permute-start(bf16[512,1]{0,1:T(2,128)(2,1)S(1)} %multiply_convert_fusion), channel_id=1, source_target_pairs={{1,0},{2,1},{3,2},{0,3},{5,4},{6,5},{7,6},{4,7},{9,8},{10,9},{11,1... | collective-permute-start | bytes 3080 | tf_op jit(solution)/shard_map/ppermute | solution.py:70
  25.4 3.6 %collective-permute-start = (bf16[512,1]{0,1:T(2,128)(2,1)S(1)}, bf16[512,1]{0,1:T(2,128)(2,1)S(1)}, u32[]{:S(2)}, u32[]{:S(2)}) collective-permute-start(bf16[512,1]{0,1:T(2,128)(2,1)S(1)} %multiply_convert_fusion), channel_id=1, source_target_pairs={{0,1},{1,2},{2,3},{3,0},{4,5},{5,6},{6,7},{7,4},{8,9},{9,10},{10,1... | collective-permute-start | bytes 3080 | tf_op jit(solution)/shard_map/ppermute | solution.py:68
  29.0 3.6 %collective-permute-start.1 = (bf16[512,1]{0,1:T(2,128)(2,1)S(1)}, bf16[512,1]{0,1:T(2,128)(2,1)S(1)}, u32[]{:S(2)}, u32[]{:S(2)}) collective-permute-start(bf16[512,1]{0,1:T(2,128)(2,1)S(1)} %collective-permute-done), channel_id=1, source_target_pairs={{0,1},{1,2},{2,3},{3,0},{4,5},{5,6},{6,7},{7,4},{8,9},{9,10},{10,1... | collective-permute-start | bytes 3080 | tf_op jit(solution)/shard_map/ppermute | solution.py:68
Sparse Core Ops, SparseCore 0:
  23.8 87.9 all-gather.1
